TPU v7x, 32 devices: a whole 2x2x4 slice. The times are simulated.
32 devices in a mesh: dp: 8 (over z, x), mp: 4 (over y, core).
Axes of the slice: x: 2, y: 2, z: 4, core: 2. Of those that a mesh axis runs over, the one named last changes fastest.
Arguments:
- patches: bfloat16 [4096, 2048], P('dp'), may hold values from -6 to 6
- cotangent: bfloat16 [4096, 8192], P('dp', 'mp'), may hold values from -0.09375 to 0.09375
- weight: float32 [2048, 8192], P('dp', 'mp'), may hold values from -0.125 to 0.125
- accum: float32 [2048, 8192], P('dp', 'mp'), may hold values from 0.1 to 4
Outputs:
- new_weight: float32 [2048, 8192], P(('dp', 'mp'))
- new_accum: float32 [2048, 8192], P(('dp', 'mp'))
- weight_copy: bfloat16 [2048, 8192], P(None, 'mp')
All inputs are finite; a program needn't handle non-finite values.
Results may differ from a plain program's by a relative error of at most 0.001.
Values may be sent and summed in bfloat16 or wider, within the bound.
A program may use at most 192 MiB of HBM per device.

v0:
```python
import jax
import jax.numpy as jnp
from jax import lax
from jax.sharding import PartitionSpec as P

learning_rate = 0.02


def adagrad(accum, weight, grad):
    summed = accum + grad * grad
    return (summed, weight - learning_rate * grad * lax.rsqrt(summed))


def shards(patches, cotangent, weight, accum):
    patch_block = lax.all_to_all(patches, "dp", split_axis=1, concat_axis=0, tiled=True)
    grad_block = jnp.einsum(
        "tr,tf->rf",
        patch_block,
        lax.all_gather(cotangent, "dp", axis=0, tiled=True),
        preferred_element_type=jnp.float32,
    )
    accum_block, weight_block = adagrad(accum, weight, grad_block)
    weight_copy = lax.all_gather(weight_block.astype(jnp.bfloat16), "dp", axis=0, tiled=True)
    new_accum, new_weight = (
        lax.all_to_all(accum_block, "mp", split_axis=0, concat_axis=1, tiled=True),
        lax.all_to_all(weight_block, "mp", split_axis=0, concat_axis=1, tiled=True),
    )
    return (new_weight, new_accum, weight_copy)


def solution(mesh):
    return jax.shard_map(
        shards,
        mesh=mesh,
        in_specs=(P("dp", None), P("dp", "mp"), P("dp", "mp"), P("dp", "mp")),
        out_specs=(P(("dp", "mp"), None), P(("dp", "mp"), None), P(None, "mp")),
        check_vma=False,
    )
```

profile of v0, /device:TPU:0, one launch (start us, length us, event | category | flops | bytes accessed | tf_op | source)
XLA Modules:
  0.0 430.2 jit_solution(2336489553796141500)
XLA Ops:
  7.2 0.0 all-gather.3.cloned.1.call-start
  7.2 0.7 all-gather.3.cloned.1.call-update
  7.9 0.0 all-gather.5.cloned.1.call-start
  7.9 2.9 copy.11
  10.8 107.2 %all_to_all.57 = bf16[512,8,256]{0,2,1:T(8,128)(2,1)} all-to-all(bf16[512,8,256]{0,2,1:T(8,128)(2,1)S(1)} %bitcast.18), channel_id=1, replica_groups=mesh['dp'=8,'mp'=4] {'dp'}, dimensions={1} | all-to-all | bytes 4194304 | tf_op jit(solution)/shard_map/all_to_all | solution.py:15
  118.0 2.8 copy.12
  120.9 158.3 %all-gather.3.cloned.1.call-done = bf16[4096,2048]{1,0:T(8,128)(2,1)} async-done(((bf16[512,2048]{1,0:T(8,128)(2,1)}), bf16[4096,2048]{1,0:T(8,128)(2,1)}) %all-gather.3.cloned.1.call-update) | async-done | bytes 16777232 | tf_op jit(solution)/shard_map/all_gather | solution.py:19
  279.1 12.9 %fusion = (bf16[256,2048]{1,0:T(8,128)(2,1)}, f32[256,2048]{1,0:T(8,128)}, f32[256,2048]{1,0:T(8,128)}) fusion(f32[256,2048]{1,0:T(8,128)} %param.6, f32[256,2048]{1,0:T(8,128)} %param.7, bf16[4096,256]{1,0:T(8,128)(2,1)S(1)} %bitcast.13, bf16[4096,2048]{1,0:T(8,128)(2,1)} %all-gather.3.cloned.1.call-done), kind=kOutput, calls=%fused_computation.2 | convolution fusion | flops 4298113024 | bytes 28311552 | tf_op jit(solution)/shard_map/tr,tf->rf/dot_general | solution.py:16
  292.0 0.0 all-gather.5.cloned.1.call-update
  292.1 30.2 %all_to_all.58 = f32[4,64,2048]{2,1,0:T(8,128)} all-to-all(f32[4,64,2048]{2,1,0:T(8,128)} %bitcast.14), channel_id=1, replica_groups=mesh['dp'=8,'mp'=4] {'mp'}, dimensions={0} | all-to-all | bytes 4194304 | tf_op jit(solution)/shard_map/all_to_all | solution.py:26
  322.2 3.6 all-to-all-start.2
  325.8 3.1 copy.15
  329.0 22.5 %all-to-all-done.2 = f32[4,64,2048]{2,1,0:T(8,128)S(1)} async-done(((f32[4,64,2048]{2,1,0:T(8,128)}), f32[4,64,2048]{2,1,0:T(8,128)S(1)}, u32[]{:S(2)}, u32[]{:S(2)}) %all-to-all-start.2) | async-done | bytes 2097184 | tf_op jit(solution)/shard_map/all_to_all | solution.py:25
  351.5 1.5 copy.16
  352.9 61.9 %all-gather.5.cloned.1.call-done = bf16[2048,2048]{1,0:T(8,128)(2,1)} async-done(((bf16[256,2048]{1,0:T(8,128)(2,1)}), bf16[2048,2048]{1,0:T(8,128)(2,1)}) %all-gather.5.cloned.1.call-update) | async-done | bytes 8388624 | tf_op jit(solution)/shard_map/all_gather | solution.py:23
  414.9 8.4 %copy.18 = bf16[2048,2048]{1,0:T(8,128)(2,1)} copy(bf16[2048,2048]{1,0:T(8,128)(2,1)} %all-gather.5.cloned.1.call-done) | data formatting | bytes 16777216
Async XLA Ops:
  7.2 272.0 %all-gather.3.cloned.1.call-start = ((), (), s32[]{:S(2)}) async-start(), calls=%async_computation.3 | async-start | bytes 18874368 | tf_op jit(solution)/shard_map/all_gather | solution.py:19
  7.9 407.0 %all-gather.5.cloned.1.call-start = ((), (), s32[]{:S(2)}) async-start(), calls=%async_computation.4 | async-start | bytes 9437184 | tf_op jit(solution)/shard_map/all_gather | solution.py:23
  322.2 29.3 %all-to-all-start.2 = ((f32[4,64,2048]{2,1,0:T(8,128)}), f32[4,64,2048]{2,1,0:T(8,128)S(1)}, u32[]{:S(2)}, u32[]{:S(2)}) async-start(f32[4,64,2048]{2,1,0:T(8,128)} %bitcast.5), calls=%async_computation.2 | async-start | bytes 4194304 | tf_op jit(solution)/shard_map/all_to_all | solution.py:25
Sparse Core Ops, SparseCore 0:
  10.1 268.9 all-gather.2
  292.2 122.6 all-gather.4
where the time goes:
time: 431 us; the launch traced here: 430 us
  waiting for transfers between devices  243 us (56%)
  blocking collectives  137 us (32%)
  local copies, waits for them, and re-layouts  18.8 us (4%)
  between operations  14.1 us (3%)
  matrix products  12.9 us (3%)
    all_gather x1, waiting for transfers between devices, shards(): lax.all_gather(cotangent, 'dp', axis=0, tiled=True)  158 us
    all_to_all x1, blocking collectives, shards(): lax.all_to_all(patches, 'dp', split_axis=1, concat_axis=0, tiled=True)  107 us
    all_gather x1, waiting for transfers between devices, shards(): lax.all_gather(weight_block.astype(jnp.bfloat16), 'dp', axis=0, tiled=True)  61.9 us
    all_to_all x1, blocking collectives, shards(): lax.all_to_all(weight_block, 'mp', split_axis=0, concat_axis=1, tiled=True)  30.2 us
    all_to_all x1, waiting for transfers between devices, shards(): lax.all_to_all(accum_block, 'mp', split_axis=0, concat_axis=1, tiled=True)  22.5 us
    dot_general x1, matrix products, shards(): jnp.einsum('tr,tf->rf', patch_block, lax.all_gather(cotangent, 'dp', axis...  12.9 us
    unnamed x2, local copies, waits for them, and re-layouts  11.3 us
  transfers between devices with their start and end apart: 3, of which 3 were waited for; matrix products, arithmetic and copies ran while one was open for 2% of the time, Pallas kernels for 0%

commit v1 on v0

--- a/solution.py
+++ b/solution.py
@@ -1,9 +1,26 @@
+import functools
 import jax
 import jax.numpy as jnp
 from jax import lax
 from jax.sharding import PartitionSpec as P
+from jax.lax import all_to_all, axis_size
 
 learning_rate = 0.02
+
+
+def remake_the_case(block_here, d0, on_dim):
+    return jnp.concatenate(
+        all_to_all(
+            jnp.stack(jnp.split(block_here, axis_size("mp"), d0), 0),
+            axis_name="mp",
+            split_axis=0,
+            concat_axis=0,
+        ),
+        on_dim,
+    )
+
+
+keep_up_weights_now = functools.partial(remake_the_case, d0=0, on_dim=1)
 
 
 def adagrad(accum, weight, grad):
@@ -22,7 +39,7 @@
     accum_block, weight_block = adagrad(accum, weight, grad_block)
     weight_copy = lax.all_gather(weight_block.astype(jnp.bfloat16), "dp", axis=0, tiled=True)
     new_accum, new_weight = (
-        lax.all_to_all(accum_block, "mp", split_axis=0, concat_axis=1, tiled=True),
+        keep_up_weights_now(accum_block),
         lax.all_to_all(weight_block, "mp", split_axis=0, concat_axis=1, tiled=True),
     )
     return (new_weight, new_accum, weight_copy)

time: 431 us -> 431 us (level)
  blocking collectives: 137 us -> 107 us
  waiting for transfers between devices: 243 us -> 267 us
  starting transfers between devices: 3.69 us -> 8.31 us
    all_to_all x1 -> x0, blocking collectives: 30.2 us -> none  [shards(): lax.all_to_all(weight_block, 'mp', split_axis=0, concat_axis=1, tiled=True)]
    all_to_all x1 -> x2, waiting for transfers between devices: 22.5 us -> 46.5 us  [the longest x1 24 us: shards(): lax.all_to_all(weight_block, 'mp', split_axis=0, concat_axis=1, tiled=True)]
    all_to_all x1 -> x2, starting transfers between devices: 3.61 us -> 8.23 us  [the longest x1 4.62 us: shards(): lax.all_to_all(weight_block, 'mp', split_axis=0, concat_axis=1, tiled=True)]
    unnamed x2 -> x4, local copies, waits for them, and re-layouts: 11.3 us -> 11.3 us
  transfers between devices with their start and end apart: 3 -> 4, of which waited for: 3 -> 4; matrix products, arithmetic and copies ran while one was open for 2% -> 3% of each run, Pallas kernels for 0% -> 0%
where the time goes in v1:
time: 431 us; the launch traced here: 430 us
  waiting for transfers between devices  267 us (62%)
  blocking collectives  107 us (25%)
  local copies, waits for them, and re-layouts  19 us (4%)
  between operations  14.1 us (3%)
  matrix products  12.9 us (3%)
  starting transfers between devices  8.31 us (2%)
    all_gather x1, waiting for transfers between devices, shards(): lax.all_gather(cotangent, 'dp', axis=0, tiled=True)  158 us
    all_to_all x1, blocking collectives, shards(): lax.all_to_all(patches, 'dp', split_axis=1, concat_axis=0, tiled=True)  107 us
    all_gather x1, waiting for transfers between devices, shards(): lax.all_gather(weight_block.astype(jnp.bfloat16), 'dp', axis=0, tiled=True)  61.7 us
    all_to_all x1, waiting for transfers between devices, shards(): lax.all_to_all(weight_block, 'mp', split_axis=0, concat_axis=1, tiled=True)  24 us
    all_to_all x1, waiting for transfers between devices, remake_the_case(): all_to_all(jnp.stack(jnp.split(block_here, axis_size('mp'), d0), 0), axis...  22.5 us
    dot_general x1, matrix products, shards(): jnp.einsum('tr,tf->rf', patch_block, lax.all_gather(cotangent, 'dp', axis...  12.9 us
    unnamed x4, local copies, waits for them, and re-layouts  11.3 us
  transfers between devices with their start and end apart: 4, of which 4 were waited for; matrix products, arithmetic and copies ran while one was open for 3% of the time, Pallas kernels for 0%

profile of v1, /device:TPU:0, one launch (start us, length us, event | category | flops | bytes accessed | tf_op | source)
XLA Modules:
  0.0 430.2 jit_solution(9312415228654659077)
XLA Ops:
  7.2 0.0 all-gather.3.cloned.1.call-start
  7.2 0.7 all-gather.3.cloned.1.call-update
  7.9 0.0 all-gather.5.cloned.1.call-start
  7.9 2.9 copy.10
  10.8 107.2 %all_to_all.43 = bf16[512,8,256]{0,2,1:T(8,128)(2,1)} all-to-all(bf16[512,8,256]{0,2,1:T(8,128)(2,1)S(1)} %bitcast.24), channel_id=1, replica_groups=mesh['dp'=8,'mp'=4] {'dp'}, dimensions={1} | all-to-all | bytes 4194304 | tf_op jit(solution)/shard_map/all_to_all | solution.py:32
  118.0 2.8 copy.11
  120.9 158.3 %all-gather.3.cloned.1.call-done = bf16[4096,2048]{1,0:T(8,128)(2,1)} async-done(((bf16[512,2048]{1,0:T(8,128)(2,1)}), bf16[4096,2048]{1,0:T(8,128)(2,1)}) %all-gather.3.cloned.1.call-update) | async-done | bytes 16777232 | tf_op jit(solution)/shard_map/all_gather | solution.py:36
  279.1 12.9 %fusion = (bf16[256,2048]{1,0:T(8,128)(2,1)}, f32[256,2048]{1,0:T(8,128)}, f32[256,2048]{1,0:T(8,128)}) fusion(f32[256,2048]{1,0:T(8,128)} %param.6, f32[256,2048]{1,0:T(8,128)} %param.7, bf16[4096,256]{1,0:T(8,128)(2,1)S(1)} %bitcast.20, bf16[4096,2048]{1,0:T(8,128)(2,1)} %all-gather.3.cloned.1.call-done), kind=kOutput, calls=%fused_computation.7 | convolution fusion | flops 4298113024 | bytes 28311552 | tf_op jit(solution)/shard_map/tr,tf->rf/dot_general | solution.py:33
  292.0 0.0 all-gather.5.cloned.1.call-update
  292.1 0.0 copy-start
  292.1 4.6 %all-to-all-start.1 = ((f32[4,64,2048]{2,1,0:T(8,128)}), f32[4,64,2048]{2,1,0:T(8,128)}, u32[]{:S(2)}, u32[]{:S(2)}) async-start(f32[4,64,2048]{2,1,0:T(8,128)} %bitcast.21), calls=%async_computation.1 | async-start | bytes 4194304 | tf_op jit(solution)/shard_map/all_to_all | solution.py:43
  296.7 0.0 copy-done
  296.7 0.2 slice_bitcast_fusion.3
  296.9 1.5 pad_maximum_fusion
  298.4 24.0 %all-to-all-done.1 = f32[4,64,2048]{2,1,0:T(8,128)} async-done(((f32[4,64,2048]{2,1,0:T(8,128)}), f32[4,64,2048]{2,1,0:T(8,128)}, u32[]{:S(2)}, u32[]{:S(2)}) %all-to-all-start.1) | async-done | bytes 2097184 | tf_op jit(solution)/shard_map/all_to_all | solution.py:43
  322.4 3.6 all-to-all-start.2
  326.1 3.1 copy.14
  329.2 22.5 %all-to-all-done.2 = f32[4,64,2048]{2,1,0:T(8,128)S(1)} async-done(((f32[4,64,2048]{2,1,0:T(8,128)}), f32[4,64,2048]{2,1,0:T(8,128)S(1)}, u32[]{:S(2)}, u32[]{:S(2)}) %all-to-all-start.2) | async-done | bytes 2097184 | tf_op jit(solution)/shard_map/all_to_all | solution.py:13
  351.7 1.5 copy.15
  353.1 61.7 %all-gather.5.cloned.1.call-done = bf16[2048,2048]{1,0:T(8,128)(2,1)} async-done(((bf16[256,2048]{1,0:T(8,128)(2,1)}), bf16[2048,2048]{1,0:T(8,128)(2,1)}) %all-gather.5.cloned.1.call-update) | async-done | bytes 8388624 | tf_op jit(solution)/shard_map/all_gather | solution.py:40
  414.9 8.4 %copy.17 = bf16[2048,2048]{1,0:T(8,128)(2,1)} copy(bf16[2048,2048]{1,0:T(8,128)(2,1)} %all-gather.5.cloned.1.call-done) | data formatting | bytes 16777216
Async XLA Ops:
  7.2 272.0 %all-gather.3.cloned.1.call-start = ((), (), s32[]{:S(2)}) async-start(), calls=%async_computation.3 | async-start | bytes 18874368 | tf_op jit(solution)/shard_map/all_gather | solution.py:36
  7.9 407.0 %all-gather.5.cloned.1.call-start = ((), (), s32[]{:S(2)}) async-start(), calls=%async_computation.4 | async-start | bytes 9437184 | tf_op jit(solution)/shard_map/all_gather | solution.py:40
  292.1 4.6 %copy-start = (f32[256,2048]{1,0:T(8,128)S(1)}, f32[256,2048]{1,0:T(8,128)}, u32[]{:S(2)}) copy-start(f32[256,2048]{1,0:T(8,128)} %get-tuple-element.5) | copy-start | bytes 6291460
  292.1 30.4 %all-to-all-start.1 = ((f32[4,64,2048]{2,1,0:T(8,128)}), f32[4,64,2048]{2,1,0:T(8,128)}, u32[]{:S(2)}, u32[]{:S(2)}) async-start(f32[4,64,2048]{2,1,0:T(8,128)} %bitcast.21), calls=%async_computation.1 | async-start | bytes 4194304 | tf_op jit(solution)/shard_map/all_to_all | solution.py:43
  322.4 29.3 %all-to-all-start.2 = ((f32[4,64,2048]{2,1,0:T(8,128)}), f32[4,64,2048]{2,1,0:T(8,128)S(1)}, u32[]{:S(2)}, u32[]{:S(2)}) async-start(f32[4,64,2048]{2,1,0:T(8,128)} %pad_maximum_fusion), calls=%async_computation.2 | async-start | bytes 4194304 | tf_op jit(solution)/shard_map/all_to_all | solution.py:13
Sparse Core Ops, SparseCore 0:
  10.1 268.9 all-gather.2
  292.2 122.6 all-gather.4

commit v2 on v0

--- a/solution.py
+++ b/solution.py
@@ -4,6 +4,22 @@
 from jax.sharding import PartitionSpec as P
 
 learning_rate = 0.02
+
+
+def summed_both_ways(array, axis, dim, product):
+    length, here, rows = (lax.axis_size(axis), lax.axis_index(axis), array.shape[dim])
+    upward = [(i, (i + 1) % length) for i in range(length)]
+    behind = [(i, (i - 1) % length) for i in range(length)]
+    half = length // 2
+    from_left = from_right = array
+    total = product(array, here * rows)
+    for step in range(1, half + 1):
+        from_left = lax.ppermute(from_left, axis, upward)
+        if step < length - half:
+            from_right = lax.ppermute(from_right, axis, behind)
+            total = total + product(from_right, (here + step) % length * rows)
+        total = total + product(from_left, (here - step) % length * rows)
+    return total
 
 
 def adagrad(accum, weight, grad):
@@ -13,11 +29,16 @@
 
 def shards(patches, cotangent, weight, accum):
     patch_block = lax.all_to_all(patches, "dp", split_axis=1, concat_axis=0, tiled=True)
-    grad_block = jnp.einsum(
-        "tr,tf->rf",
-        patch_block,
-        lax.all_gather(cotangent, "dp", axis=0, tiled=True),
-        preferred_element_type=jnp.float32,
+    grad_block = summed_both_ways(
+        cotangent,
+        "dp",
+        0,
+        lambda part, offset: jnp.einsum(
+            "tr,tf->rf",
+            lax.dynamic_slice_in_dim(patch_block, offset, part.shape[0], axis=0),
+            part,
+            preferred_element_type=jnp.float32,
+        ),
     )
     accum_block, weight_block = adagrad(accum, weight, grad_block)
     weight_copy = lax.all_gather(weight_block.astype(jnp.bfloat16), "dp", axis=0, tiled=True)

time: 431 us -> 499 us (1.16)
  waiting for transfers between devices: 243 us -> 392 us
  blocking collectives: 137 us -> 28.9 us
  starting transfers between devices: 3.69 us -> 26.4 us
    ppermute x0 -> x7, waiting for transfers between devices: none -> 302 us  [the longest x4 182 us: summed_both_ways(): from_left = lax.ppermute(from_left, axis, upward)]
    all_gather x1 -> x0, waiting for transfers between devices: 158 us -> none  [shards(): lax.all_gather(cotangent, 'dp', axis=0, tiled=True)]
    all_to_all x1 -> x0, blocking collectives: 107 us -> none  [shards(): lax.all_to_all(patches, 'dp', split_axis=1, concat_axis=0, tiled=True)]
    ppermute x0 -> x7, starting transfers between devices: none -> 17.9 us  [the longest x4 10.1 us: summed_both_ways(): from_left = lax.ppermute(from_left, axis, upward)]
    dot_general x1 -> x8, matrix products: 12.9 us -> 17.8 us  [shards(): jnp.einsum('tr,tf->rf', lax.dynamic_slice_in_dim(patch_block, offset, par...]
    unnamed x2 -> x8, local copies, waits for them, and re-layouts: 11.3 us -> 12.4 us
  transfers between devices with their start and end apart: 3 -> 10, of which waited for: 3 -> 7; matrix products, arithmetic and copies ran while one was open for 2% -> 5% of each run, Pallas kernels for 0% -> 0%
where the time goes in v2:
time: 499 us; the launch traced here: 498 us
  waiting for transfers between devices  392 us (79%)
  blocking collectives  28.9 us (6%)
  starting transfers between devices  26.4 us (5%)
  local copies, waits for them, and re-layouts  19.4 us (4%)
  matrix products  17.8 us (4%)
  between operations  14.1 us (3%)
    ppermute x4, waiting for transfers between devices, summed_both_ways(): from_left = lax.ppermute(from_left, axis, upward)  182 us
    ppermute x3, waiting for transfers between devices, summed_both_ways(): from_right = lax.ppermute(from_right, axis, behind)  121 us
    all_gather x1, waiting for transfers between devices, shards(): lax.all_gather(weight_block.astype(jnp.bfloat16), 'dp', axis=0, tiled=True)  63.7 us
    all_to_all x1, blocking collectives, shards(): lax.all_to_all(weight_block, 'mp', split_axis=0, concat_axis=1, tiled=True)  28.9 us
    all_to_all x1, waiting for transfers between devices, shards(): lax.all_to_all(accum_block, 'mp', split_axis=0, concat_axis=1, tiled=True)  22.5 us
    dot_general x8, matrix products, shards(): jnp.einsum('tr,tf->rf', lax.dynamic_slice_in_dim(patch_block, offset, par...  17.8 us
    unnamed x8, local copies, waits for them, and re-layouts  12.4 us
    ppermute x4, starting transfers between devices, summed_both_ways(): from_left = lax.ppermute(from_left, axis, upward)  10.1 us
  transfers between devices with their start and end apart: 10, of which 7 were waited for; matrix products, arithmetic and copies ran while one was open for 5% of the time, Pallas kernels for 0%

profile of v2, /device:TPU:0, one launch (start us, length us, event | category | flops | bytes accessed | tf_op | source)
XLA Modules:
  0.0 498.4 jit_solution(15570328939333143267)
XLA Ops:
  7.2 3.0 collective-permute-start.1
  10.2 3.1 collective-permute-start
  13.3 87.0 %collective-permute-done.1 = bf16[512,2048]{1,0:T(8,128)(2,1)} collective-permute-done((bf16[512,2048]{1,0:T(8,128)(2,1)}, bf16[512,2048]{1,0:T(8,128)(2,1)}, u32[]{:S(2)}, u32[]{:S(2)}) %collective-permute-start.1) | collective-permute-done | bytes 2097184 | tf_op jit(solution)/shard_map/ppermute | solution.py:17
  100.3 2.5 collective-permute-start.3
  102.8 3.9 copy.11
  106.7 4.9 all-to-all-start
  111.6 0.0 all-gather.2.cloned.1.call-start
  111.6 0.0 collective-permute-done
  111.7 4.7 collective-permute-start.2
  116.4 94.6 %collective-permute-done.3 = bf16[512,2048]{1,0:T(8,128)(2,1)} collective-permute-done((bf16[512,2048]{1,0:T(8,128)(2,1)}, bf16[512,2048]{1,0:T(8,128)(2,1)}, u32[]{:S(2)}, u32[]{:S(2)}) %collective-permute-start.3) | collective-permute-done | bytes 2097184 | tf_op jit(solution)/shard_map/ppermute | solution.py:17
  210.9 2.5 collective-permute-start.5
  213.4 3.1 all-to-all-done
  216.6 2.4 copy.12
  218.9 44.4 %collective-permute-done.2 = bf16[512,2048]{1,0:T(8,128)(2,1)} collective-permute-done((bf16[512,2048]{1,0:T(8,128)(2,1)}, bf16[512,2048]{1,0:T(8,128)(2,1)}, u32[]{:S(2)}, u32[]{:S(2)}) %collective-permute-start.2) | collective-permute-done | bytes 2097184 | tf_op jit(solution)/shard_map/ppermute | solution.py:19
  263.3 0.0 collective-permute-start.4
  263.3 0.0 copy-start
  263.3 2.5 fusion.11
  265.8 0.0 collective-permute-done.5
  265.9 2.1 collective-permute-start.6
  267.9 0.0 copy-done
  267.9 2.3 convolution_add_fusion.4
  270.3 2.3 convolution_add_fusion.3
  272.6 2.3 fusion.6
  275.0 2.4 fusion.1
  277.3 2.3 fusion.3
  279.6 0.0 copy-start.1
  279.7 0.0 copy-start.2
  279.7 76.3 %collective-permute-done.4 = bf16[512,2048]{1,0:T(8,128)(2,1)S(1)} collective-permute-done((bf16[512,2048]{1,0:T(8,128)(2,1)}, bf16[512,2048]{1,0:T(8,128)(2,1)S(1)}, u32[]{:S(2)}, u32[]{:S(2)}) %collective-permute-start.4) | collective-permute-done | bytes 2097184 | tf_op jit(solution)/shard_map/ppermute | solution.py:19
  356.0 0.8 fusion
  356.8 0.0 collective-permute-done.6
  356.8 0.0 copy-done.1
  356.8 0.0 copy-done.2
  356.9 2.7 fusion.21
  359.6 0.0 all-gather.2.cloned.1.call-update
  359.6 28.9 %all_to_all.57 = f32[4,64,2048]{2,1,0:T(8,128)} all-to-all(f32[4,64,2048]{2,1,0:T(8,128)S(1)} %bitcast.32), channel_id=1, replica_groups=mesh['dp'=8,'mp'=4] {'mp'}, dimensions={0} | all-to-all | bytes 4194304 | tf_op jit(solution)/shard_map/all_to_all | solution.py:47
  388.6 3.6 all-to-all-start.2
  392.2 3.2 copy.15
  395.3 22.5 %all-to-all-done.2 = f32[4,64,2048]{2,1,0:T(8,128)S(1)} async-done(((f32[4,64,2048]{2,1,0:T(8,128)}), f32[4,64,2048]{2,1,0:T(8,128)S(1)}, u32[]{:S(2)}, u32[]{:S(2)}) %all-to-all-start.2) | async-done | bytes 2097184 | tf_op jit(solution)/shard_map/all_to_all | solution.py:46
  417.8 1.5 copy.16
  419.4 63.7 %all-gather.2.cloned.1.call-done = bf16[2048,2048]{1,0:T(8,128)(2,1)} async-done(((bf16[256,2048]{1,0:T(8,128)(2,1)}), bf16[2048,2048]{1,0:T(8,128)(2,1)}) %all-gather.2.cloned.1.call-update) | async-done | bytes 8388624 | tf_op jit(solution)/shard_map/all_gather | solution.py:44
  483.1 8.4 %copy.18 = bf16[2048,2048]{1,0:T(8,128)(2,1)} copy(bf16[2048,2048]{1,0:T(8,128)(2,1)} %all-gather.2.cloned.1.call-done) | data formatting | bytes 16777216
Async XLA Ops:
  7.2 93.2 %collective-permute-start.1 = (bf16[512,2048]{1,0:T(8,128)(2,1)}, bf16[512,2048]{1,0:T(8,128)(2,1)}, u32[]{:S(2)}, u32[]{:S(2)}) collective-permute-start(bf16[512,2048]{1,0:T(8,128)(2,1)} %param.5), channel_id=1, source_target_pairs={{0,4},{4,8},{8,12},{12,16},{16,20},{20,24},{24,28},{28,0},{1,5},{5... | collective-permute-start | bytes 6291464 | tf_op jit(solution)/shard_map/ppermute | solution.py:17
  10.2 101.5 %collective-permute-start = (bf16[512,2048]{1,0:T(8,128)(2,1)}, bf16[512,2048]{1,0:T(8,128)(2,1)}, u32[]{:S(2)}, u32[]{:S(2)}) collective-permute-start(bf16[512,2048]{1,0:T(8,128)(2,1)} %param.5), channel_id=1, source_target_pairs={{0,28},{4,0},{8,4},{12,8},{16,12},{20,16},{24,20},{28,24},{1,29},{... | collective-permute-start | bytes 6291464 | tf_op jit(solution)/shard_map/ppermute | solution.py:19
  100.3 110.6 %collective-permute-start.3 = (bf16[512,2048]{1,0:T(8,128)(2,1)}, bf16[512,2048]{1,0:T(8,128)(2,1)}, u32[]{:S(2)}, u32[]{:S(2)}) collective-permute-start(bf16[512,2048]{1,0:T(8,128)(2,1)} %collective-permute-done.1), channel_id=1, source_target_pairs={{0,4},{4,8},{8,12},{12,16},{16,20},{20,24},{24,28},{28,0},{1,5},{5... | collective-permute-start | bytes 6291464 | tf_op jit(solution)/shard_map/ppermute | solution.py:17
  106.7 109.8 %all-to-all-start = ((bf16[512,8,256]{0,2,1:T(8,128)(2,1)}), bf16[512,8,256]{0,2,1:T(8,128)(2,1)S(1)}, u32[]{:S(2)}, u32[]{:S(2)}) async-start(bf16[512,8,256]{0,2,1:T(8,128)(2,1)} %bitcast.20), calls=%async_computation | async-start | bytes 4194304 | tf_op jit(solution)/shard_map/all_to_all | solution.py:31
  111.6 371.5 %all-gather.2.cloned.1.call-start = ((), (), s32[]{:S(2)}) async-start(), calls=%async_computation.3 | async-start | bytes 9437184 | tf_op jit(solution)/shard_map/all_gather | solution.py:44
  111.7 151.6 %collective-permute-start.2 = (bf16[512,2048]{1,0:T(8,128)(2,1)}, bf16[512,2048]{1,0:T(8,128)(2,1)}, u32[]{:S(2)}, u32[]{:S(2)}) collective-permute-start(bf16[512,2048]{1,0:T(8,128)(2,1)} %collective-permute-done), channel_id=1, source_target_pairs={{0,28},{4,0},{8,4},{12,8},{16,12},{20,16},{24,20},{28,24},{1,29},{... | collective-permute-start | bytes 6291464 | tf_op jit(solution)/shard_map/ppermute | solution.py:19
  210.9 54.9 %collective-permute-start.5 = (bf16[512,2048]{1,0:T(8,128)(2,1)}, bf16[512,2048]{1,0:T(8,128)(2,1)}, u32[]{:S(2)}, u32[]{:S(2)}) collective-permute-start(bf16[512,2048]{1,0:T(8,128)(2,1)} %collective-permute-done.3), channel_id=1, source_target_pairs={{0,4},{4,8},{8,12},{12,16},{16,20},{20,24},{24,28},{28,0},{1,5},{5... | collective-permute-start | bytes 6291464 | tf_op jit(solution)/shard_map/ppermute | solution.py:17
  263.3 92.7 %collective-permute-start.4 = (bf16[512,2048]{1,0:T(8,128)(2,1)}, bf16[512,2048]{1,0:T(8,128)(2,1)S(1)}, u32[]{:S(2)}, u32[]{:S(2)}) collective-permute-start(bf16[512,2048]{1,0:T(8,128)(2,1)} %collective-permute-done.2), channel_id=1, source_target_pairs={{0,28},{4,0},{8,4},{12,8},{16,12},{20,16},{24,20},{28,24},{1,29},{... | collective-permute-start | bytes 6291464 | tf_op jit(solution)/shard_map/ppermute | solution.py:19
  263.3 4.6 copy-start
  265.9 91.0 %collective-permute-start.6 = (bf16[512,2048]{1,0:T(8,128)(2,1)}, bf16[512,2048]{1,0:T(8,128)(2,1)S(1)}, u32[]{:S(2)}, u32[]{:S(2)}) collective-permute-start(bf16[512,2048]{1,0:T(8,128)(2,1)} %collective-permute-done.5), channel_id=1, source_target_pairs={{0,4},{4,8},{8,12},{12,16},{16,20},{20,24},{24,28},{28,0},{1,5},{5... | collective-permute-start | bytes 6291464 | tf_op jit(solution)/shard_map/ppermute | solution.py:17
  279.6 77.2 %copy-start.1 = (f32[256,2048]{1,0:T(8,128)S(1)}, f32[256,2048]{1,0:T(8,128)}, u32[]{:S(2)}) copy-start(f32[256,2048]{1,0:T(8,128)} %param.6) | copy-start | bytes 6291460
  279.7 77.2 %copy-start.2 = (f32[256,2048]{1,0:T(8,128)S(1)}, f32[256,2048]{1,0:T(8,128)}, u32[]{:S(2)}) copy-start(f32[256,2048]{1,0:T(8,128)} %param.7) | copy-start | bytes 6291460
  388.6 29.3 %all-to-all-start.2 = ((f32[4,64,2048]{2,1,0:T(8,128)}), f32[4,64,2048]{2,1,0:T(8,128)S(1)}, u32[]{:S(2)}, u32[]{:S(2)}) async-start(f32[4,64,2048]{2,1,0:T(8,128)} %bitcast.31), calls=%async_computation.2 | async-start | bytes 4194304 | tf_op jit(solution)/shard_map/all_to_all | solution.py:46
Sparse Core Ops, SparseCore 0:
  359.7 123.2 all-gather.1
